TPU v7x, 32 devices: a whole 2x2x4 slice. The times are simulated.
32 devices in a mesh: gx: 4 (over y, x), gy: 2 (over core), gz: 4 (over z).
Axes of the slice: x: 2, y: 2, z: 4, core: 2. Of those that a mesh axis runs over, the one named last changes fastest.
Arguments:
- residual_in: float32 [256, 128, 1024], P('gx', 'gy', 'gz'), may hold values from -700 to 700
Outputs:
- level_one: float32 [128, 64, 512], P('gx', 'gy', 'gz')
- level_two: float32 [64, 32, 256], P('gx', 'gy', 'gz')
- level_three: float32 [32, 16, 128], P('gx', 'gy', 'gz')
- level_four: float32 [16, 8, 64], P('gx', 'gy', 'gz')
- level_five: float32 [8, 4, 32], P('gx', 'gy', 'gz')
- level_scales: float32 [5], replicated
All inputs are finite; a program needn't handle non-finite values.
Results may differ from a plain program's by a relative error of at most 0.0002.
Values sent between devices are 32-bit elements; how exact they have to be, the bound alone decides.
A program may use at most 64 MiB of HBM per device.

v0:
```python
import jax
import jax.numpy as jnp
from jax import lax
from jax.sharding import PartitionSpec as P

LEVELS = 5
EPSILON = 1e-06


def shifted(block, axis, distance):
    devices = range(lax.axis_size(axis))
    route = [(i - distance, i) for i in devices if i - distance in devices]
    return lax.ppermute(block, axis, route)


def pass_axis(values, axis_pos, rim_plane):
    length = values.shape[axis_pos]
    half = length // 2
    if axis_pos == 2:
        rows = lax.broadcasted_iota(jnp.int32, (length, half), 0)
        cols = lax.broadcasted_iota(jnp.int32, (length, half), 1)
        table = jnp.where(
            rows == 2 * cols,
            0.5,
            jnp.where((rows == 2 * cols + 1) | (rows == 2 * cols - 1), 0.25, 0.0),
        ).astype(jnp.float32)
        reduced = lax.dot_general(
            values,
            table,
            (((2,), (0,)), ((), ())),
            precision=lax.Precision.HIGHEST,
            preferred_element_type=jnp.float32,
        )
        tail = jnp.zeros(values.shape[:2] + (half - 1,), jnp.float32)
        return reduced + jnp.concatenate([0.25 * rim_plane, tail], axis=2)
    new_shape = values.shape[:axis_pos] + (half, 2) + values.shape[axis_pos + 1 :]
    paired = values.reshape(new_shape)
    even_part = lax.index_in_dim(paired, 0, axis_pos + 1, False)
    odd_part = lax.index_in_dim(paired, 1, axis_pos + 1, False)
    earlier = jnp.concatenate(
        [rim_plane, lax.slice_in_dim(odd_part, 0, half - 1, 1, axis_pos)], axis=axis_pos
    )
    return 0.5 * even_part + 0.25 * odd_part + 0.25 * earlier


def extend_cube(values):
    plane_x = shifted(values[-1:, :, :], "gx", 1)
    values = jnp.concatenate([plane_x, values], axis=0)
    plane_y = shifted(values[:, -1:, :], "gy", 1)
    values = jnp.concatenate([plane_y, values], axis=1)
    plane_z = shifted(values[:, :, -1:], "gz", 1)
    return jnp.concatenate([plane_z, values], axis=2)


def combine_cube(padded):
    values = pass_axis(padded[1:], 0, padded[:1])
    values = pass_axis(values[:, 1:], 1, values[:, :1])
    return pass_axis(values[:, :, 1:], 2, values[:, :, :1])


def restrict_any(values):
    return combine_cube(extend_cube(values))


def per_device(residual_in):
    devices_all = lax.axis_size("gx") * lax.axis_size("gy") * lax.axis_size("gz")
    current = residual_in
    grid_list = []
    scale_list = []
    unscaled = []
    sums_local = []
    for step_no in range(LEVELS):
        coarse = restrict_any(current)
        sums_local.append(jnp.sum(coarse * coarse))
        unscaled.append(coarse)
        current = coarse
    totals = lax.psum(jnp.stack(sums_local), ("gx", "gy", "gz"))
    product = jnp.float32(1.0)
    for step_no in range(LEVELS):
        cells = unscaled[step_no].size * devices_all
        scale_now = jnp.sqrt(totals[step_no] / (product * product) / cells + EPSILON)
        product = product * scale_now
        grid_list.append(unscaled[step_no] / product)
        scale_list.append(scale_now)
    return (
        grid_list[0],
        grid_list[1],
        grid_list[2],
        grid_list[3],
        grid_list[4],
        jnp.stack(scale_list),
    )


def solution(mesh):
    placed = (P("gx", "gy", "gz"),)
    return jax.shard_map(
        per_device,
        mesh=mesh,
        in_specs=placed,
        out_specs=(
            P("gx", "gy", "gz"),
            P("gx", "gy", "gz"),
            P("gx", "gy", "gz"),
            P("gx", "gy", "gz"),
            P("gx", "gy", "gz"),
            P(),
        ),
        check_vma=False,
    )
```

profile of v0, /device:TPU:0, one launch (start us, length us, event | category | flops | bytes accessed | tf_op | source)
XLA Modules:
  0.0 157.5 jit_solution(14000450861790597113)
XLA Ops:
  1.5 4.9 %collective-permute-start = (f32[1,64,256]{2,1,0:T(8,128)S(1)}, f32[1,64,256]{2,1,0:T(8,128)S(1)}, u32[]{:S(2)}, u32[]{:S(2)}) collective-permute-start(f32[1,64,256]{2,1,0:T(8,128)S(1)} %slice.260), channel_id=1, source_target_pairs={{0,8},{8,16},{16,24},{1,9},{9,17},{17,25},{2,10},{10,18},{18,26},{... | collective-permute-start | bytes 196616 | tf_op jit(solution)/shard_map/ppermute | solution.py:13
  6.3 1.9 %collective-permute-done = f32[1,64,256]{2,1,0:T(8,128)S(1)} collective-permute-done((f32[1,64,256]{2,1,0:T(8,128)S(1)}, f32[1,64,256]{2,1,0:T(8,128)S(1)}, u32[]{:S(2)}, u32[]{:S(2)}) %collective-permute-start) | collective-permute-done | bytes 65568 | tf_op jit(solution)/shard_map/ppermute | solution.py:13
  8.2 3.0 %constant_dynamic-update-slice_fusion = f32[65,64,256]{2,1,0:T(8,128)S(1)} fusion(f32[65,64,256]{2,1,0:T(8,128)S(1)} %constant_dynamic-update-slice_fusion.1, f32[64,64,256]{2,1,0:T(8,128)} %param.1), kind=kLoop, calls=%fused_computation.182 | loop fusion | bytes 8388608 | tf_op jit(solution)/shard_map/concatenate | solution.py:48
  11.3 1.3 collective-permute-start.1
  15.1 3.5 %collective-permute-start.2 = (f32[65,65,1]{1,2,0:T(1,128)S(1)}, f32[65,65,1]{1,2,0:T(1,128)S(1)}, u32[]{:S(2)}, u32[]{:S(2)}) collective-permute-start(f32[65,65,1]{1,2,0:T(1,128)S(1)} %copy.49), channel_id=1, source_target_pairs={{0,1},{1,2},{2,3},{4,5},{5,6},{6,7},{8,9},{9,10},{10,11},{12,13},{... | collective-permute-start | bytes 50708 | tf_op jit(solution)/shard_map/ppermute | solution.py:13
  18.6 1.6 collective-permute-done.2
  21.1 4.7 %maximum_maximum_fusion = f32[65,65,257]{2,1,0:T(8,128)S(1)} fusion(f32[65,64,256]{2,1,0:T(8,128)} %copy-done, f32[65,1,256]{2,1,0:T(1,128)S(1)} %collective-permute-done.1, f32[65,65,1]{2,1,0:T(8,128)S(1)} %copy.50), kind=kLoop, calls=%fused_computation | loop fusion | flops 2171650 | bytes 8686600 | tf_op jit(solution)/shard_map/concatenate | solution.py:52
  26.6 2.1 %fusion.2 = f32[32,65,257]{2,1,0:T(8,128)S(1)} fusion(f32[65,65,1]{2,1,0:T(8,128)S(1)} %copy.50, f32[65,64,256]{2,1,0:T(8,128)S(1)} %bitcast.209, f32[65,1,256]{2,1,0:T(1,128)S(1)} %collective-permute-done.1, f32[32,2,65,257]{3,2,1,0:T(8,128)S(1)} %bitcast.207, f32[31,65,257]{2,1,0:T(8,128)S(1)} %slice_bitcast_fusion.2), kind=kLoop, calls=%fused_computation.4 | loop fusion | flops 6414720 | bytes 12829440 | tf_op jit(solution)/shard_map/add | solution.py:43
  29.2 1.8 %copy.55 = f32[32,64,257]{2,0,1:T(8,128)S(1)} copy(f32[32,64,257]{2,1,0:T(8,128)S(1)} %slice.350) | data formatting | bytes 4210688 | tf_op jit(solution)/shard_map/slice | solution.py:57
  32.2 2.0 %fusion.10 = f32[32,32,257]{2,1,0:T(8,128)S(1)} fusion(f32[32,31,257]{2,1,0:T(8,128)S(1)} %bitcast.213, f32[32,1,257]{2,1,0:T(1,128)S(1)} %slice.353, f32[32,32,1,257]{3,0,2,1:T(8,128)S(1)} %get-tuple-element.6, f32[32,32,1,257]{3,0,2,1:T(8,128)S(1)} %get-tuple-element.7), kind=kLoop, calls=%fused_computation.18 | loop fusion | flops 1579008 | bytes 4210688 | tf_op jit(solution)/shard_map/add | solution.py:43
  34.2 1.6 %multiply_reduce_fusion = (f32[]{:T(128)}, f32[32,32,128]{2,1,0:T(8,128)S(1)}) fusion(f32[32,32,1]{2,1,0:T(8,128)S(1)} %slice_multiply_fusion, s32[128]{0:T(128)S(1)} %get-tuple-element.34, s32[128]{0:T(128)S(1)} %broadcast_add_fusion.9, s32[128]{0:T(128)S(1)} %get-tuple-element.33, f32[32,32,257]{2,1,0:T(8,128)S(1)} %fusion.10), kind=kOutput, calls=%fused_computation.49 | convolution fusion | flops 403243008 | bytes 2098692 | tf_op jit(solution)/shard_map/dot_general | solution.py:27
  35.9 4.3 %collective-permute-start.3 = (f32[1,32,128]{2,1,0:T(8,128)S(1)}, f32[1,32,128]{2,1,0:T(8,128)S(1)}, u32[]{:S(2)}, u32[]{:S(2)}) collective-permute-start(f32[1,32,128]{2,1,0:T(8,128)S(1)} %slice.357), channel_id=1, source_target_pairs={{0,8},{8,16},{16,24},{1,9},{9,17},{17,25},{2,10},{10,18},{18,26},{... | collective-permute-start | bytes 49160 | tf_op jit(solution)/shard_map/ppermute | solution.py:13
  40.1 1.4 collective-permute-done.3
  41.6 1.3 collective-permute-start.4
  44.3 4.4 %collective-permute-start.5 = (f32[33,33,1]{1,2,0:T(1,128)S(1)}, f32[33,33,1]{1,2,0:T(1,128)S(1)}, u32[]{:S(2)}, u32[]{:S(2)}) collective-permute-start(f32[33,33,1]{1,2,0:T(1,128)S(1)} %copy.58), channel_id=1, source_target_pairs={{0,1},{1,2},{2,3},{4,5},{5,6},{6,7},{8,9},{9,10},{10,11},{12,13},{... | collective-permute-start | bytes 13076 | tf_op jit(solution)/shard_map/ppermute | solution.py:13
  53.0 4.3 %collective-permute-start.6 = (f32[1,16,64]{2,1,0:T(8,128)S(1)}, f32[1,16,64]{2,1,0:T(8,128)S(1)}, u32[]{:S(2)}, u32[]{:S(2)}) collective-permute-start(f32[1,16,64]{2,1,0:T(8,128)S(1)} %slice.369), channel_id=1, source_target_pairs={{0,8},{8,16},{16,24},{1,9},{9,17},{17,25},{2,10},{10,18},{18,26},{... | collective-permute-start | bytes 12296 | tf_op jit(solution)/shard_map/ppermute | solution.py:13
  57.3 1.3 collective-permute-done.6
  58.7 1.3 collective-permute-start.7
  60.9 4.2 %collective-permute-start.8 = (f32[17,17,1]{2,1,0:T(8,128)S(1)}, f32[17,17,1]{2,1,0:T(8,128)S(1)}, u32[]{:S(2)}, u32[]{:S(2)}) collective-permute-start(f32[17,17,1]{2,1,0:T(8,128)S(1)} %pad_maximum_fusion.3), channel_id=1, source_target_pairs={{0,1},{1,2},{2,3},{4,5},{5,6},{6,7},{8,9},{9,10},{10,11},{12,13},{... | collective-permute-start | bytes 3476 | tf_op jit(solution)/shard_map/ppermute | solution.py:13
  65.1 4.9 %collective-permute-done.8 = f32[17,17,1]{2,1,0:T(8,128)S(1)} collective-permute-done((f32[17,17,1]{2,1,0:T(8,128)S(1)}, f32[17,17,1]{2,1,0:T(8,128)S(1)}, u32[]{:S(2)}, u32[]{:S(2)}) %collective-permute-start.8) | collective-permute-done | bytes 1188 | tf_op jit(solution)/shard_map/ppermute | solution.py:13
  71.3 5.1 %collective-permute-start.9 = (f32[1,8,32]{2,1,0:T(8,128)S(1)}, f32[1,8,32]{2,1,0:T(8,128)S(1)}, u32[]{:S(2)}, u32[]{:S(2)}) collective-permute-start(f32[1,8,32]{2,1,0:T(8,128)S(1)} %slice.381), channel_id=1, source_target_pairs={{0,8},{8,16},{16,24},{1,9},{9,17},{17,25},{2,10},{10,18},{18,26},{... | collective-permute-start | bytes 3080 | tf_op jit(solution)/shard_map/ppermute | solution.py:13
  76.4 1.3 collective-permute-done.9
  77.7 1.3 collective-permute-start.10
  79.9 4.4 %collective-permute-start.11 = (f32[9,9,1]{2,1,0:T(8,128)S(1)}, f32[9,9,1]{2,1,0:T(8,128)S(1)}, u32[]{:S(2)}, u32[]{:S(2)}) collective-permute-start(f32[9,9,1]{2,1,0:T(8,128)S(1)} %pad_maximum_fusion.5), channel_id=1, source_target_pairs={{0,1},{1,2},{2,3},{4,5},{5,6},{6,7},{8,9},{9,10},{10,11},{12,13},{... | collective-permute-start | bytes 980 | tf_op jit(solution)/shard_map/ppermute | solution.py:13
  84.3 2.0 %collective-permute-done.11 = f32[9,9,1]{2,1,0:T(8,128)S(1)} collective-permute-done((f32[9,9,1]{2,1,0:T(8,128)S(1)}, f32[9,9,1]{2,1,0:T(8,128)S(1)}, u32[]{:S(2)}, u32[]{:S(2)}) %collective-permute-start.11) | collective-permute-done | bytes 356 | tf_op jit(solution)/shard_map/ppermute | solution.py:13
  87.5 5.1 %collective-permute-start.12 = (f32[1,4,16]{2,1,0:T(4,128)S(1)}, f32[1,4,16]{2,1,0:T(4,128)S(1)}, u32[]{:S(2)}, u32[]{:S(2)}) collective-permute-start(f32[1,4,16]{2,1,0:T(4,128)S(1)} %slice.393), channel_id=1, source_target_pairs={{0,8},{8,16},{16,24},{1,9},{9,17},{17,25},{2,10},{10,18},{18,26},{... | collective-permute-start | bytes 776 | tf_op jit(solution)/shard_map/ppermute | solution.py:13
  92.5 1.3 collective-permute-done.12
  93.8 1.3 collective-permute-start.13
  96.0 4.4 %collective-permute-start.14 = (f32[5,5,1]{2,1,0:T(8,128)S(1)}, f32[5,5,1]{2,1,0:T(8,128)S(1)}, u32[]{:S(2)}, u32[]{:S(2)}) collective-permute-start(f32[5,5,1]{2,1,0:T(8,128)S(1)} %pad_maximum_fusion.7), channel_id=1, source_target_pairs={{0,1},{1,2},{2,3},{4,5},{5,6},{6,7},{8,9},{9,10},{10,11},{12,13},{... | collective-permute-start | bytes 308 | tf_op jit(solution)/shard_map/ppermute | solution.py:13
  100.4 1.5 collective-permute-done.14
  103.0 3.3 %stack.39 = f32[5]{0:T(128)S(1)} concatenate(f32[1]{0:T(128)} %bitcast.7, f32[1]{0:T(128)} %bitcast.15, f32[1]{0:T(128)} %bitcast.23, f32[1]{0:T(128)} %bitcast.31, f32[1]{0:T(128)} %bitcast.39), dimensions={0} | concatenate | bytes 40 | tf_op jit(solution)/shard_map/stack | solution.py:77
  106.3 43.1 %psum.7 = f32[5]{0:T(128)S(1)} all-reduce(f32[5]{0:T(128)S(1)} %stack.39), channel_id=1, replica_groups=mesh['gx'=4,'gy'=2,'gz'=4] {'gx','gy','gz'}, use_global_device_ids=true, to_apply=%region_5.6 | all-reduce | flops 5 | bytes 40 | tf_op jit(solution)/shard_map/psum | solution.py:77
  (105 shorter events, 23.0 us)
Async XLA Ops:
  1.5 6.8 %collective-permute-start = (f32[1,64,256]{2,1,0:T(8,128)S(1)}, f32[1,64,256]{2,1,0:T(8,128)S(1)}, u32[]{:S(2)}, u32[]{:S(2)}) collective-permute-start(f32[1,64,256]{2,1,0:T(8,128)S(1)} %slice.260), channel_id=1, source_target_pairs={{0,8},{8,16},{16,24},{1,9},{9,17},{17,25},{2,10},{10,18},{18,26},{... | collective-permute-start | bytes 196616 | tf_op jit(solution)/shard_map/ppermute | solution.py:13
  11.2 2.3 %copy-start = (f32[65,64,256]{2,1,0:T(8,128)}, f32[65,64,256]{2,1,0:T(8,128)S(1)}, u32[]{:S(2)}) copy-start(f32[65,64,256]{2,1,0:T(8,128)S(1)} %constant_dynamic-update-slice_fusion) | copy-start | bytes 12779524
  11.3 2.2 %collective-permute-start.1 = (f32[65,1,256]{2,1,0:T(1,128)S(1)}, f32[65,1,256]{2,1,0:T(1,128)S(1)}, u32[]{:S(2)}, u32[]{:S(2)}) collective-permute-start(f32[65,1,256]{2,1,0:T(1,128)S(1)} %slice.345), channel_id=1, source_target_pairs={{0,4},{1,5},{2,6},{3,7},{8,12},{9,13},{10,14},{11,15},{16,20},{17,... | collective-permute-start | bytes 199688 | tf_op jit(solution)/shard_map/ppermute | solution.py:13
  15.1 5.1 %collective-permute-start.2 = (f32[65,65,1]{1,2,0:T(1,128)S(1)}, f32[65,65,1]{1,2,0:T(1,128)S(1)}, u32[]{:S(2)}, u32[]{:S(2)}) collective-permute-start(f32[65,65,1]{1,2,0:T(1,128)S(1)} %copy.49), channel_id=1, source_target_pairs={{0,1},{1,2},{2,3},{4,5},{5,6},{6,7},{8,9},{9,10},{10,11},{12,13},{... | collective-permute-start | bytes 50708 | tf_op jit(solution)/shard_map/ppermute | solution.py:13
  21.1 5.4 %slice-start = ((s8[4259840]{0:T(1024)(128)(4,1)}), s8[4194304]{0:T(1024)(128)(4,1)S(1)}, s32[]{:S(2)}) async-start(s8[4259840]{0:T(1024)(128)(4,1)} %bitcast.208), calls=%async_computation | async-start | bytes 8388608
  25.8 0.8 slice-start.1
  35.9 5.7 %collective-permute-start.3 = (f32[1,32,128]{2,1,0:T(8,128)S(1)}, f32[1,32,128]{2,1,0:T(8,128)S(1)}, u32[]{:S(2)}, u32[]{:S(2)}) collective-permute-start(f32[1,32,128]{2,1,0:T(8,128)S(1)} %slice.357), channel_id=1, source_target_pairs={{0,8},{8,16},{16,24},{1,9},{9,17},{17,25},{2,10},{10,18},{18,26},{... | collective-permute-start | bytes 49160 | tf_op jit(solution)/shard_map/ppermute | solution.py:13
  41.6 2.1 %collective-permute-start.4 = (f32[33,1,128]{2,1,0:T(1,128)S(1)}, f32[33,1,128]{2,1,0:T(1,128)S(1)}, u32[]{:S(2)}, u32[]{:S(2)}) collective-permute-start(f32[33,1,128]{2,1,0:T(1,128)S(1)} %pad_maximum_fusion.9), channel_id=1, source_target_pairs={{0,4},{1,5},{2,6},{3,7},{8,12},{9,13},{10,14},{11,15},{16,20},{17,... | collective-permute-start | bytes 50696 | tf_op jit(solution)/shard_map/ppermute | solution.py:13
  44.3 5.7 %collective-permute-start.5 = (f32[33,33,1]{1,2,0:T(1,128)S(1)}, f32[33,33,1]{1,2,0:T(1,128)S(1)}, u32[]{:S(2)}, u32[]{:S(2)}) collective-permute-start(f32[33,33,1]{1,2,0:T(1,128)S(1)} %copy.58), channel_id=1, source_target_pairs={{0,1},{1,2},{2,3},{4,5},{5,6},{6,7},{8,9},{9,10},{10,11},{12,13},{... | collective-permute-start | bytes 13076 | tf_op jit(solution)/shard_map/ppermute | solution.py:13
  53.0 5.6 %collective-permute-start.6 = (f32[1,16,64]{2,1,0:T(8,128)S(1)}, f32[1,16,64]{2,1,0:T(8,128)S(1)}, u32[]{:S(2)}, u32[]{:S(2)}) collective-permute-start(f32[1,16,64]{2,1,0:T(8,128)S(1)} %slice.369), channel_id=1, source_target_pairs={{0,8},{8,16},{16,24},{1,9},{9,17},{17,25},{2,10},{10,18},{18,26},{... | collective-permute-start | bytes 12296 | tf_op jit(solution)/shard_map/ppermute | solution.py:13
  58.7 2.1 %collective-permute-start.7 = (f32[17,1,64]{2,1,0:T(1,128)S(1)}, f32[17,1,64]{2,1,0:T(1,128)S(1)}, u32[]{:S(2)}, u32[]{:S(2)}) collective-permute-start(f32[17,1,64]{2,1,0:T(1,128)S(1)} %pad_maximum_fusion.10), channel_id=1, source_target_pairs={{0,4},{1,5},{2,6},{3,7},{8,12},{9,13},{10,14},{11,15},{16,20},{17,... | collective-permute-start | bytes 13064 | tf_op jit(solution)/shard_map/ppermute | solution.py:13
  60.9 9.1 %collective-permute-start.8 = (f32[17,17,1]{2,1,0:T(8,128)S(1)}, f32[17,17,1]{2,1,0:T(8,128)S(1)}, u32[]{:S(2)}, u32[]{:S(2)}) collective-permute-start(f32[17,17,1]{2,1,0:T(8,128)S(1)} %pad_maximum_fusion.3), channel_id=1, source_target_pairs={{0,1},{1,2},{2,3},{4,5},{5,6},{6,7},{8,9},{9,10},{10,11},{12,13},{... | collective-permute-start | bytes 3476 | tf_op jit(solution)/shard_map/ppermute | solution.py:13
  71.3 6.4 %collective-permute-start.9 = (f32[1,8,32]{2,1,0:T(8,128)S(1)}, f32[1,8,32]{2,1,0:T(8,128)S(1)}, u32[]{:S(2)}, u32[]{:S(2)}) collective-permute-start(f32[1,8,32]{2,1,0:T(8,128)S(1)} %slice.381), channel_id=1, source_target_pairs={{0,8},{8,16},{16,24},{1,9},{9,17},{17,25},{2,10},{10,18},{18,26},{... | collective-permute-start | bytes 3080 | tf_op jit(solution)/shard_map/ppermute | solution.py:13
  77.7 2.1 %collective-permute-start.10 = (f32[9,1,32]{2,1,0:T(1,128)S(1)}, f32[9,1,32]{2,1,0:T(1,128)S(1)}, u32[]{:S(2)}, u32[]{:S(2)}) collective-permute-start(f32[9,1,32]{2,1,0:T(1,128)S(1)} %pad_maximum_fusion.11), channel_id=1, source_target_pairs={{0,4},{1,5},{2,6},{3,7},{8,12},{9,13},{10,14},{11,15},{16,20},{17,... | collective-permute-start | bytes 3464 | tf_op jit(solution)/shard_map/ppermute | solution.py:13
  79.9 6.4 %collective-permute-start.11 = (f32[9,9,1]{2,1,0:T(8,128)S(1)}, f32[9,9,1]{2,1,0:T(8,128)S(1)}, u32[]{:S(2)}, u32[]{:S(2)}) collective-permute-start(f32[9,9,1]{2,1,0:T(8,128)S(1)} %pad_maximum_fusion.5), channel_id=1, source_target_pairs={{0,1},{1,2},{2,3},{4,5},{5,6},{6,7},{8,9},{9,10},{10,11},{12,13},{... | collective-permute-start | bytes 980 | tf_op jit(solution)/shard_map/ppermute | solution.py:13
  87.5 6.4 %collective-permute-start.12 = (f32[1,4,16]{2,1,0:T(4,128)S(1)}, f32[1,4,16]{2,1,0:T(4,128)S(1)}, u32[]{:S(2)}, u32[]{:S(2)}) collective-permute-start(f32[1,4,16]{2,1,0:T(4,128)S(1)} %slice.393), channel_id=1, source_target_pairs={{0,8},{8,16},{16,24},{1,9},{9,17},{17,25},{2,10},{10,18},{18,26},{... | collective-permute-start | bytes 776 | tf_op jit(solution)/shard_map/ppermute | solution.py:13
  93.8 2.1 %collective-permute-start.13 = (f32[5,1,16]{2,1,0:T(1,128)S(1)}, f32[5,1,16]{2,1,0:T(1,128)S(1)}, u32[]{:S(2)}, u32[]{:S(2)}) collective-permute-start(f32[5,1,16]{2,1,0:T(1,128)S(1)} %pad_maximum_fusion.12), channel_id=1, source_target_pairs={{0,4},{1,5},{2,6},{3,7},{8,12},{9,13},{10,14},{11,15},{16,20},{17,... | collective-permute-start | bytes 968 | tf_op jit(solution)/shard_map/ppermute | solution.py:13
  96.0 5.9 %collective-permute-start.14 = (f32[5,5,1]{2,1,0:T(8,128)S(1)}, f32[5,5,1]{2,1,0:T(8,128)S(1)}, u32[]{:S(2)}, u32[]{:S(2)}) collective-permute-start(f32[5,5,1]{2,1,0:T(8,128)S(1)} %pad_maximum_fusion.7), channel_id=1, source_target_pairs={{0,1},{1,2},{2,3},{4,5},{5,6},{6,7},{8,9},{9,10},{10,11},{12,13},{... | collective-permute-start | bytes 308 | tf_op jit(solution)/shard_map/ppermute | solution.py:13
where the time goes:
time: 158 us; the launch traced here: 157 us
  starting transfers between devices  50.9 us (32%)
  blocking collectives  43.1 us (27%)
  waiting for transfers between devices  22.5 us (14%)
  local copies, waits for them, and re-layouts  15.9 us (10%)
  other arithmetic  15.3 us (10%)
  matrix products  5.1 us (3%)
  between operations  4.72 us (3%)
    ppermute x15, starting transfers between devices, shifted(): return lax.ppermute(block, axis, route)  50.9 us
    psum x1, blocking collectives, per_device(): totals = lax.psum(jnp.stack(sums_local), ('gx', 'gy', 'gz'))  43.1 us
    ppermute x15, waiting for transfers between devices, shifted(): return lax.ppermute(block, axis, route)  22.5 us
    concatenate x5, other arithmetic, extend_cube(): return jnp.concatenate([plane_z, values], axis=2)  5.51 us
    dot_general x5, matrix products, pass_axis(): lax.dot_general(values, table, (((2,), (0,)), ((), ())), precision=lax.Pr...  5.1 us
    add x10, other arithmetic, pass_axis(): return 0.5 * even_part + 0.25 * odd_part + 0.25 * earlier  4.91 us
    div x5, other arithmetic, per_device(): grid_list.append(unscaled[step_no] / product)  3.34 us
    another operation x1, local copies, waits for them, and re-layouts, per_device(): totals = lax.psum(jnp.stack(sums_local), ('gx', 'gy', 'gz'))  3.31 us
  transfers between devices with their start and end apart: 15, of which 15 were waited for; matrix products, arithmetic and copies ran while one was open for 0% of the time, Pallas kernels for 0%

commit v1 on v0

--- a/solution.py
+++ b/solution.py
@@ -74,7 +74,7 @@
         sums_local.append(jnp.sum(coarse * coarse))
         unscaled.append(coarse)
         current = coarse
-    totals = lax.psum(jnp.stack(sums_local), ("gx", "gy", "gz"))
+    totals = lax.psum(lax.psum(jnp.stack(sums_local), ("gy", "gz")), "gx")
     product = jnp.float32(1.0)
     for step_no in range(LEVELS):
         cells = unscaled[step_no].size * devices_all

time: 158 us -> 143 us (0.905)
  blocking collectives: 43.1 us -> 27.7 us
    psum x1 -> x2, blocking collectives: 43.1 us -> 27.7 us  [per_device(): totals = lax.psum(lax.psum(jnp.stack(sums_local), ('gy', 'gz')), 'gx')]
where the time goes in v1:
time: 143 us; the launch traced here: 142 us
  starting transfers between devices  50.9 us (36%)
  blocking collectives  27.7 us (19%)
  waiting for transfers between devices  22.5 us (16%)
  local copies, waits for them, and re-layouts  15.9 us (11%)
  other arithmetic  15.3 us (11%)
  matrix products  5.1 us (4%)
  between operations  4.72 us (3%)
    ppermute x15, starting transfers between devices, shifted(): return lax.ppermute(block, axis, route)  50.9 us
    psum x2, blocking collectives, per_device(): totals = lax.psum(lax.psum(jnp.stack(sums_local), ('gy', 'gz')), 'gx')  27.7 us
    ppermute x15, waiting for transfers between devices, shifted(): return lax.ppermute(block, axis, route)  22.5 us
    concatenate x5, other arithmetic, extend_cube(): return jnp.concatenate([plane_z, values], axis=2)  5.51 us
    dot_general x5, matrix products, pass_axis(): lax.dot_general(values, table, (((2,), (0,)), ((), ())), precision=lax.Pr...  5.1 us
    add x10, other arithmetic, pass_axis(): return 0.5 * even_part + 0.25 * odd_part + 0.25 * earlier  4.91 us
    div x5, other arithmetic, per_device(): grid_list.append(unscaled[step_no] / product)  3.34 us
    another operation x1, local copies, waits for them, and re-layouts, per_device(): totals = lax.psum(lax.psum(jnp.stack(sums_local), ('gy', 'gz')), 'gx')  3.31 us
  transfers between devices with their start and end apart: 15, of which 15 were waited for; matrix products, arithmetic and copies ran while one was open for 0% of the time, Pallas kernels for 0%

profile of v1, /device:TPU:0, one launch (start us, length us, event | category | flops | bytes accessed | tf_op | source)
XLA Modules:
  0.0 142.0 jit_solution(15272526762301315228)
XLA Ops:
  1.5 4.9 %collective-permute-start = (f32[1,64,256]{2,1,0:T(8,128)S(1)}, f32[1,64,256]{2,1,0:T(8,128)S(1)}, u32[]{:S(2)}, u32[]{:S(2)}) collective-permute-start(f32[1,64,256]{2,1,0:T(8,128)S(1)} %slice.260), channel_id=1, source_target_pairs={{0,8},{8,16},{16,24},{1,9},{9,17},{17,25},{2,10},{10,18},{18,26},{... | collective-permute-start | bytes 196616 | tf_op jit(solution)/shard_map/ppermute | solution.py:13
  6.3 1.9 %collective-permute-done = f32[1,64,256]{2,1,0:T(8,128)S(1)} collective-permute-done((f32[1,64,256]{2,1,0:T(8,128)S(1)}, f32[1,64,256]{2,1,0:T(8,128)S(1)}, u32[]{:S(2)}, u32[]{:S(2)}) %collective-permute-start) | collective-permute-done | bytes 65568 | tf_op jit(solution)/shard_map/ppermute | solution.py:13
  8.2 3.0 %constant_dynamic-update-slice_fusion = f32[65,64,256]{2,1,0:T(8,128)S(1)} fusion(f32[65,64,256]{2,1,0:T(8,128)S(1)} %constant_dynamic-update-slice_fusion.1, f32[64,64,256]{2,1,0:T(8,128)} %param.1), kind=kLoop, calls=%fused_computation.182 | loop fusion | bytes 8388608 | tf_op jit(solution)/shard_map/concatenate | solution.py:48
  11.3 1.3 collective-permute-start.1
  15.1 3.5 %collective-permute-start.2 = (f32[65,65,1]{1,2,0:T(1,128)S(1)}, f32[65,65,1]{1,2,0:T(1,128)S(1)}, u32[]{:S(2)}, u32[]{:S(2)}) collective-permute-start(f32[65,65,1]{1,2,0:T(1,128)S(1)} %copy.49), channel_id=1, source_target_pairs={{0,1},{1,2},{2,3},{4,5},{5,6},{6,7},{8,9},{9,10},{10,11},{12,13},{... | collective-permute-start | bytes 50708 | tf_op jit(solution)/shard_map/ppermute | solution.py:13
  18.6 1.6 %collective-permute-done.2 = f32[65,65,1]{1,2,0:T(1,128)S(1)} collective-permute-done((f32[65,65,1]{1,2,0:T(1,128)S(1)}, f32[65,65,1]{1,2,0:T(1,128)S(1)}, u32[]{:S(2)}, u32[]{:S(2)}) %collective-permute-start.2) | collective-permute-done | bytes 16932 | tf_op jit(solution)/shard_map/ppermute | solution.py:13
  21.1 4.7 %maximum_maximum_fusion = f32[65,65,257]{2,1,0:T(8,128)S(1)} fusion(f32[65,64,256]{2,1,0:T(8,128)} %copy-done, f32[65,1,256]{2,1,0:T(1,128)S(1)} %collective-permute-done.1, f32[65,65,1]{2,1,0:T(8,128)S(1)} %copy.50), kind=kLoop, calls=%fused_computation | loop fusion | flops 2171650 | bytes 8686600 | tf_op jit(solution)/shard_map/concatenate | solution.py:52
  26.6 2.1 %fusion.2 = f32[32,65,257]{2,1,0:T(8,128)S(1)} fusion(f32[65,65,1]{2,1,0:T(8,128)S(1)} %copy.50, f32[65,64,256]{2,1,0:T(8,128)S(1)} %bitcast.209, f32[65,1,256]{2,1,0:T(1,128)S(1)} %collective-permute-done.1, f32[32,2,65,257]{3,2,1,0:T(8,128)S(1)} %bitcast.207, f32[31,65,257]{2,1,0:T(8,128)S(1)} %slice_bitcast_fusion.2), kind=kLoop, calls=%fused_computation.4 | loop fusion | flops 6414720 | bytes 12829440 | tf_op jit(solution)/shard_map/add | solution.py:43
  29.2 1.8 %copy.55 = f32[32,64,257]{2,0,1:T(8,128)S(1)} copy(f32[32,64,257]{2,1,0:T(8,128)S(1)} %slice.350) | data formatting | bytes 4210688 | tf_op jit(solution)/shard_map/slice | solution.py:57
  32.2 2.0 %fusion.10 = f32[32,32,257]{2,1,0:T(8,128)S(1)} fusion(f32[32,31,257]{2,1,0:T(8,128)S(1)} %bitcast.213, f32[32,1,257]{2,1,0:T(1,128)S(1)} %slice.353, f32[32,32,1,257]{3,0,2,1:T(8,128)S(1)} %get-tuple-element.6, f32[32,32,1,257]{3,0,2,1:T(8,128)S(1)} %get-tuple-element.7), kind=kLoop, calls=%fused_computation.18 | loop fusion | flops 1579008 | bytes 4210688 | tf_op jit(solution)/shard_map/add | solution.py:43
  34.2 1.6 %multiply_reduce_fusion = (f32[]{:T(128)}, f32[32,32,128]{2,1,0:T(8,128)S(1)}) fusion(f32[32,32,1]{2,1,0:T(8,128)S(1)} %slice_multiply_fusion, s32[128]{0:T(128)S(1)} %get-tuple-element.34, s32[128]{0:T(128)S(1)} %broadcast_add_fusion.9, s32[128]{0:T(128)S(1)} %get-tuple-element.33, f32[32,32,257]{2,1,0:T(8,128)S(1)} %fusion.10), kind=kOutput, calls=%fused_computation.49 | convolution fusion | flops 403243008 | bytes 2098692 | tf_op jit(solution)/shard_map/dot_general | solution.py:27
  35.9 4.3 %collective-permute-start.3 = (f32[1,32,128]{2,1,0:T(8,128)S(1)}, f32[1,32,128]{2,1,0:T(8,128)S(1)}, u32[]{:S(2)}, u32[]{:S(2)}) collective-permute-start(f32[1,32,128]{2,1,0:T(8,128)S(1)} %slice.357), channel_id=1, source_target_pairs={{0,8},{8,16},{16,24},{1,9},{9,17},{17,25},{2,10},{10,18},{18,26},{... | collective-permute-start | bytes 49160 | tf_op jit(solution)/shard_map/ppermute | solution.py:13
  40.1 1.4 %collective-permute-done.3 = f32[1,32,128]{2,1,0:T(8,128)S(1)} collective-permute-done((f32[1,32,128]{2,1,0:T(8,128)S(1)}, f32[1,32,128]{2,1,0:T(8,128)S(1)}, u32[]{:S(2)}, u32[]{:S(2)}) %collective-permute-start.3) | collective-permute-done | bytes 16416 | tf_op jit(solution)/shard_map/ppermute | solution.py:13
  41.6 1.3 collective-permute-start.4
  44.3 4.4 %collective-permute-start.5 = (f32[33,33,1]{1,2,0:T(1,128)S(1)}, f32[33,33,1]{1,2,0:T(1,128)S(1)}, u32[]{:S(2)}, u32[]{:S(2)}) collective-permute-start(f32[33,33,1]{1,2,0:T(1,128)S(1)} %copy.58), channel_id=1, source_target_pairs={{0,1},{1,2},{2,3},{4,5},{5,6},{6,7},{8,9},{9,10},{10,11},{12,13},{... | collective-permute-start | bytes 13076 | tf_op jit(solution)/shard_map/ppermute | solution.py:13
  53.0 4.3 %collective-permute-start.6 = (f32[1,16,64]{2,1,0:T(8,128)S(1)}, f32[1,16,64]{2,1,0:T(8,128)S(1)}, u32[]{:S(2)}, u32[]{:S(2)}) collective-permute-start(f32[1,16,64]{2,1,0:T(8,128)S(1)} %slice.369), channel_id=1, source_target_pairs={{0,8},{8,16},{16,24},{1,9},{9,17},{17,25},{2,10},{10,18},{18,26},{... | collective-permute-start | bytes 12296 | tf_op jit(solution)/shard_map/ppermute | solution.py:13
  57.3 1.3 collective-permute-done.6
  58.7 1.3 collective-permute-start.7
  60.9 4.2 %collective-permute-start.8 = (f32[17,17,1]{2,1,0:T(8,128)S(1)}, f32[17,17,1]{2,1,0:T(8,128)S(1)}, u32[]{:S(2)}, u32[]{:S(2)}) collective-permute-start(f32[17,17,1]{2,1,0:T(8,128)S(1)} %pad_maximum_fusion.3), channel_id=1, source_target_pairs={{0,1},{1,2},{2,3},{4,5},{5,6},{6,7},{8,9},{9,10},{10,11},{12,13},{... | collective-permute-start | bytes 3476 | tf_op jit(solution)/shard_map/ppermute | solution.py:13
  65.1 4.9 %collective-permute-done.8 = f32[17,17,1]{2,1,0:T(8,128)S(1)} collective-permute-done((f32[17,17,1]{2,1,0:T(8,128)S(1)}, f32[17,17,1]{2,1,0:T(8,128)S(1)}, u32[]{:S(2)}, u32[]{:S(2)}) %collective-permute-start.8) | collective-permute-done | bytes 1188 | tf_op jit(solution)/shard_map/ppermute | solution.py:13
  71.3 5.1 %collective-permute-start.9 = (f32[1,8,32]{2,1,0:T(8,128)S(1)}, f32[1,8,32]{2,1,0:T(8,128)S(1)}, u32[]{:S(2)}, u32[]{:S(2)}) collective-permute-start(f32[1,8,32]{2,1,0:T(8,128)S(1)} %slice.381), channel_id=1, source_target_pairs={{0,8},{8,16},{16,24},{1,9},{9,17},{17,25},{2,10},{10,18},{18,26},{... | collective-permute-start | bytes 3080 | tf_op jit(solution)/shard_map/ppermute | solution.py:13
  76.4 1.3 collective-permute-done.9
  77.7 1.3 collective-permute-start.10
  79.9 4.4 %collective-permute-start.11 = (f32[9,9,1]{2,1,0:T(8,128)S(1)}, f32[9,9,1]{2,1,0:T(8,128)S(1)}, u32[]{:S(2)}, u32[]{:S(2)}) collective-permute-start(f32[9,9,1]{2,1,0:T(8,128)S(1)} %pad_maximum_fusion.5), channel_id=1, source_target_pairs={{0,1},{1,2},{2,3},{4,5},{5,6},{6,7},{8,9},{9,10},{10,11},{12,13},{... | collective-permute-start | bytes 980 | tf_op jit(solution)/shard_map/ppermute | solution.py:13
  84.3 2.0 %collective-permute-done.11 = f32[9,9,1]{2,1,0:T(8,128)S(1)} collective-permute-done((f32[9,9,1]{2,1,0:T(8,128)S(1)}, f32[9,9,1]{2,1,0:T(8,128)S(1)}, u32[]{:S(2)}, u32[]{:S(2)}) %collective-permute-start.11) | collective-permute-done | bytes 356 | tf_op jit(solution)/shard_map/ppermute | solution.py:13
  87.5 5.1 %collective-permute-start.12 = (f32[1,4,16]{2,1,0:T(4,128)S(1)}, f32[1,4,16]{2,1,0:T(4,128)S(1)}, u32[]{:S(2)}, u32[]{:S(2)}) collective-permute-start(f32[1,4,16]{2,1,0:T(4,128)S(1)} %slice.393), channel_id=1, source_target_pairs={{0,8},{8,16},{16,24},{1,9},{9,17},{17,25},{2,10},{10,18},{18,26},{... | collective-permute-start | bytes 776 | tf_op jit(solution)/shard_map/ppermute | solution.py:13
  92.5 1.3 collective-permute-done.12
  96.0 4.4 %collective-permute-start.14 = (f32[5,5,1]{2,1,0:T(8,128)S(1)}, f32[5,5,1]{2,1,0:T(8,128)S(1)}, u32[]{:S(2)}, u32[]{:S(2)}) collective-permute-start(f32[5,5,1]{2,1,0:T(8,128)S(1)} %pad_maximum_fusion.7), channel_id=1, source_target_pairs={{0,1},{1,2},{2,3},{4,5},{5,6},{6,7},{8,9},{9,10},{10,11},{12,13},{... | collective-permute-start | bytes 308 | tf_op jit(solution)/shard_map/ppermute | solution.py:13
  100.4 1.5 %collective-permute-done.14 = f32[5,5,1]{2,1,0:T(8,128)S(1)} collective-permute-done((f32[5,5,1]{2,1,0:T(8,128)S(1)}, f32[5,5,1]{2,1,0:T(8,128)S(1)}, u32[]{:S(2)}, u32[]{:S(2)}) %collective-permute-start.14) | collective-permute-done | bytes 132 | tf_op jit(solution)/shard_map/ppermute | solution.py:13
  103.0 3.3 %stack.39 = f32[5]{0:T(128)S(1)} concatenate(f32[1]{0:T(128)} %bitcast.7, f32[1]{0:T(128)} %bitcast.15, f32[1]{0:T(128)} %bitcast.23, f32[1]{0:T(128)} %bitcast.31, f32[1]{0:T(128)} %bitcast.39), dimensions={0} | concatenate | bytes 40 | tf_op jit(solution)/shard_map/stack | solution.py:77
  106.3 16.8 %psum.14 = f32[5]{0:T(128)S(1)} all-reduce(f32[5]{0:T(128)S(1)} %stack.39), channel_id=1, replica_groups=mesh['gx'=4,'gy'=2,'gz'=4] {'gy','gz'}, use_global_device_ids=true, to_apply=%region_5.6 | all-reduce | flops 5 | bytes 40 | tf_op jit(solution)/shard_map/psum | solution.py:77
  123.1 10.9 %psum.15 = f32[5]{0:T(128)S(1)} all-reduce(f32[5]{0:T(128)S(1)} %psum.14), channel_id=1, replica_groups=mesh['gx'=4,'gy'=2,'gz'=4] {'gx'}, use_global_device_ids=true, to_apply=%region_6.7 | all-reduce | flops 5 | bytes 40 | tf_op jit(solution)/shard_map/psum | solution.py:77
  (106 shorter events, 24.3 us)
Async XLA Ops:
  1.5 6.8 %collective-permute-start = (f32[1,64,256]{2,1,0:T(8,128)S(1)}, f32[1,64,256]{2,1,0:T(8,128)S(1)}, u32[]{:S(2)}, u32[]{:S(2)}) collective-permute-start(f32[1,64,256]{2,1,0:T(8,128)S(1)} %slice.260), channel_id=1, source_target_pairs={{0,8},{8,16},{16,24},{1,9},{9,17},{17,25},{2,10},{10,18},{18,26},{... | collective-permute-start | bytes 196616 | tf_op jit(solution)/shard_map/ppermute | solution.py:13
  11.2 2.3 %copy-start = (f32[65,64,256]{2,1,0:T(8,128)}, f32[65,64,256]{2,1,0:T(8,128)S(1)}, u32[]{:S(2)}) copy-start(f32[65,64,256]{2,1,0:T(8,128)S(1)} %constant_dynamic-update-slice_fusion) | copy-start | bytes 12779524
  11.3 2.2 %collective-permute-start.1 = (f32[65,1,256]{2,1,0:T(1,128)S(1)}, f32[65,1,256]{2,1,0:T(1,128)S(1)}, u32[]{:S(2)}, u32[]{:S(2)}) collective-permute-start(f32[65,1,256]{2,1,0:T(1,128)S(1)} %slice.345), channel_id=1, source_target_pairs={{0,4},{1,5},{2,6},{3,7},{8,12},{9,13},{10,14},{11,15},{16,20},{17,... | collective-permute-start | bytes 199688 | tf_op jit(solution)/shard_map/ppermute | solution.py:13
  15.1 5.1 %collective-permute-start.2 = (f32[65,65,1]{1,2,0:T(1,128)S(1)}, f32[65,65,1]{1,2,0:T(1,128)S(1)}, u32[]{:S(2)}, u32[]{:S(2)}) collective-permute-start(f32[65,65,1]{1,2,0:T(1,128)S(1)} %copy.49), channel_id=1, source_target_pairs={{0,1},{1,2},{2,3},{4,5},{5,6},{6,7},{8,9},{9,10},{10,11},{12,13},{... | collective-permute-start | bytes 50708 | tf_op jit(solution)/shard_map/ppermute | solution.py:13
  21.1 5.4 %slice-start = ((s8[4259840]{0:T(1024)(128)(4,1)}), s8[4194304]{0:T(1024)(128)(4,1)S(1)}, s32[]{:S(2)}) async-start(s8[4259840]{0:T(1024)(128)(4,1)} %bitcast.208), calls=%async_computation | async-start | bytes 8388608
  25.8 0.8 slice-start.1
  35.9 5.7 %collective-permute-start.3 = (f32[1,32,128]{2,1,0:T(8,128)S(1)}, f32[1,32,128]{2,1,0:T(8,128)S(1)}, u32[]{:S(2)}, u32[]{:S(2)}) collective-permute-start(f32[1,32,128]{2,1,0:T(8,128)S(1)} %slice.357), channel_id=1, source_target_pairs={{0,8},{8,16},{16,24},{1,9},{9,17},{17,25},{2,10},{10,18},{18,26},{... | collective-permute-start | bytes 49160 | tf_op jit(solution)/shard_map/ppermute | solution.py:13
  41.6 2.1 %collective-permute-start.4 = (f32[33,1,128]{2,1,0:T(1,128)S(1)}, f32[33,1,128]{2,1,0:T(1,128)S(1)}, u32[]{:S(2)}, u32[]{:S(2)}) collective-permute-start(f32[33,1,128]{2,1,0:T(1,128)S(1)} %pad_maximum_fusion.9), channel_id=1, source_target_pairs={{0,4},{1,5},{2,6},{3,7},{8,12},{9,13},{10,14},{11,15},{16,20},{17,... | collective-permute-start | bytes 50696 | tf_op jit(solution)/shard_map/ppermute | solution.py:13
  44.3 5.7 %collective-permute-start.5 = (f32[33,33,1]{1,2,0:T(1,128)S(1)}, f32[33,33,1]{1,2,0:T(1,128)S(1)}, u32[]{:S(2)}, u32[]{:S(2)}) collective-permute-start(f32[33,33,1]{1,2,0:T(1,128)S(1)} %copy.58), channel_id=1, source_target_pairs={{0,1},{1,2},{2,3},{4,5},{5,6},{6,7},{8,9},{9,10},{10,11},{12,13},{... | collective-permute-start | bytes 13076 | tf_op jit(solution)/shard_map/ppermute | solution.py:13
  53.0 5.6 %collective-permute-start.6 = (f32[1,16,64]{2,1,0:T(8,128)S(1)}, f32[1,16,64]{2,1,0:T(8,128)S(1)}, u32[]{:S(2)}, u32[]{:S(2)}) collective-permute-start(f32[1,16,64]{2,1,0:T(8,128)S(1)} %slice.369), channel_id=1, source_target_pairs={{0,8},{8,16},{16,24},{1,9},{9,17},{17,25},{2,10},{10,18},{18,26},{... | collective-permute-start | bytes 12296 | tf_op jit(solution)/shard_map/ppermute | solution.py:13
  58.7 2.1 %collective-permute-start.7 = (f32[17,1,64]{2,1,0:T(1,128)S(1)}, f32[17,1,64]{2,1,0:T(1,128)S(1)}, u32[]{:S(2)}, u32[]{:S(2)}) collective-permute-start(f32[17,1,64]{2,1,0:T(1,128)S(1)} %pad_maximum_fusion.10), channel_id=1, source_target_pairs={{0,4},{1,5},{2,6},{3,7},{8,12},{9,13},{10,14},{11,15},{16,20},{17,... | collective-permute-start | bytes 13064 | tf_op jit(solution)/shard_map/ppermute | solution.py:13
  60.9 9.1 %collective-permute-start.8 = (f32[17,17,1]{2,1,0:T(8,128)S(1)}, f32[17,17,1]{2,1,0:T(8,128)S(1)}, u32[]{:S(2)}, u32[]{:S(2)}) collective-permute-start(f32[17,17,1]{2,1,0:T(8,128)S(1)} %pad_maximum_fusion.3), channel_id=1, source_target_pairs={{0,1},{1,2},{2,3},{4,5},{5,6},{6,7},{8,9},{9,10},{10,11},{12,13},{... | collective-permute-start | bytes 3476 | tf_op jit(solution)/shard_map/ppermute | solution.py:13
  71.3 6.4 %collective-permute-start.9 = (f32[1,8,32]{2,1,0:T(8,128)S(1)}, f32[1,8,32]{2,1,0:T(8,128)S(1)}, u32[]{:S(2)}, u32[]{:S(2)}) collective-permute-start(f32[1,8,32]{2,1,0:T(8,128)S(1)} %slice.381), channel_id=1, source_target_pairs={{0,8},{8,16},{16,24},{1,9},{9,17},{17,25},{2,10},{10,18},{18,26},{... | collective-permute-start | bytes 3080 | tf_op jit(solution)/shard_map/ppermute | solution.py:13
  77.7 2.1 %collective-permute-start.10 = (f32[9,1,32]{2,1,0:T(1,128)S(1)}, f32[9,1,32]{2,1,0:T(1,128)S(1)}, u32[]{:S(2)}, u32[]{:S(2)}) collective-permute-start(f32[9,1,32]{2,1,0:T(1,128)S(1)} %pad_maximum_fusion.11), channel_id=1, source_target_pairs={{0,4},{1,5},{2,6},{3,7},{8,12},{9,13},{10,14},{11,15},{16,20},{17,... | collective-permute-start | bytes 3464 | tf_op jit(solution)/shard_map/ppermute | solution.py:13
  79.9 6.4 %collective-permute-start.11 = (f32[9,9,1]{2,1,0:T(8,128)S(1)}, f32[9,9,1]{2,1,0:T(8,128)S(1)}, u32[]{:S(2)}, u32[]{:S(2)}) collective-permute-start(f32[9,9,1]{2,1,0:T(8,128)S(1)} %pad_maximum_fusion.5), channel_id=1, source_target_pairs={{0,1},{1,2},{2,3},{4,5},{5,6},{6,7},{8,9},{9,10},{10,11},{12,13},{... | collective-permute-start | bytes 980 | tf_op jit(solution)/shard_map/ppermute | solution.py:13
  87.5 6.4 %collective-permute-start.12 = (f32[1,4,16]{2,1,0:T(4,128)S(1)}, f32[1,4,16]{2,1,0:T(4,128)S(1)}, u32[]{:S(2)}, u32[]{:S(2)}) collective-permute-start(f32[1,4,16]{2,1,0:T(4,128)S(1)} %slice.393), channel_id=1, source_target_pairs={{0,8},{8,16},{16,24},{1,9},{9,17},{17,25},{2,10},{10,18},{18,26},{... | collective-permute-start | bytes 776 | tf_op jit(solution)/shard_map/ppermute | solution.py:13
  93.8 2.1 %collective-permute-start.13 = (f32[5,1,16]{2,1,0:T(1,128)S(1)}, f32[5,1,16]{2,1,0:T(1,128)S(1)}, u32[]{:S(2)}, u32[]{:S(2)}) collective-permute-start(f32[5,1,16]{2,1,0:T(1,128)S(1)} %pad_maximum_fusion.12), channel_id=1, source_target_pairs={{0,4},{1,5},{2,6},{3,7},{8,12},{9,13},{10,14},{11,15},{16,20},{17,... | collective-permute-start | bytes 968 | tf_op jit(solution)/shard_map/ppermute | solution.py:13
  96.0 5.9 %collective-permute-start.14 = (f32[5,5,1]{2,1,0:T(8,128)S(1)}, f32[5,5,1]{2,1,0:T(8,128)S(1)}, u32[]{:S(2)}, u32[]{:S(2)}) collective-permute-start(f32[5,5,1]{2,1,0:T(8,128)S(1)} %pad_maximum_fusion.7), channel_id=1, source_target_pairs={{0,1},{1,2},{2,3},{4,5},{5,6},{6,7},{8,9},{9,10},{10,11},{12,13},{... | collective-permute-start | bytes 308 | tf_op jit(solution)/shard_map/ppermute | solution.py:13
